TPU v7x, 32 devices: a whole 2x2x4 slice. The times are simulated.
32 devices in a mesh: row: 8 (over z, core), col: 4 (over y, x).
Axes of the slice: x: 2, y: 2, z: 4, core: 2. Of those that a mesh axis runs over, the one named last changes fastest.
Arguments:
- tokens: bfloat16 [16384, 6144], P(('row', 'col')), may hold values from -6 to 6
- grad_out: bfloat16 [16384, 6144], P(('row', 'col')), may hold values from -6 to 6
- w_up: bfloat16 [6144, 512], replicated, may hold values from -0.078125 to 0.078125
- w_down: bfloat16 [512, 6144], replicated, may hold values from -0.0390625 to 0.0390625
Outputs:
- up_grad: float32 [6144, 512], P('row', 'col')
- down_grad: float32 [6144, 512], P('row', 'col')
All inputs are finite; a program needn't handle non-finite values.
Results may differ from a plain program's by a relative error of at most 0.0041.
Values may be sent and summed in bfloat16 or wider, within the bound.
A program may use at most 128 MiB of HBM per device.

v0:
```python
import math

import jax
import jax.numpy as jnp
from jax import lax
from jax.sharding import PartitionSpec as P


def gelu_parts(preact):
    cumul = 0.5 * (1.0 + jax.scipy.special.erf(preact / math.sqrt(2.0)))
    density = jnp.exp(-0.5 * preact * preact) / math.sqrt(2.0 * math.pi)
    return (preact * cumul, cumul + preact * density)


def reduce_bucket(term):
    levels = term.astype(jnp.bfloat16)
    rows, cols = levels.shape
    col_count = lax.axis_size("col")
    piece_cols = cols // col_count
    got_levels = lax.all_to_all(
        levels.reshape(rows, col_count, piece_cols), "col", split_axis=1, concat_axis=1, tiled=True
    )
    partial_sum = jnp.sum(got_levels, axis=1, dtype=jnp.float32)
    return lax.psum_scatter(partial_sum, "row", scatter_dimension=0, tiled=True)


def local(tokens, grad_out, w_up, w_down):
    preact = jnp.dot(tokens, w_up, preferred_element_type=jnp.float32)
    act_grad = lax.dot_general(
        grad_out, w_down, (((1,), (1,)), ((), ())), preferred_element_type=jnp.float32
    )
    value, slope = gelu_parts(preact)
    act = value.astype(jnp.bfloat16)
    hidden_grad = (act_grad * slope).astype(jnp.bfloat16)
    term_up = lax.dot_general(
        tokens, hidden_grad, (((0,), (0,)), ((), ())), preferred_element_type=jnp.float32
    )
    summed_up = reduce_bucket(term_up)
    term_down = lax.dot_general(
        grad_out, act, (((0,), (0,)), ((), ())), preferred_element_type=jnp.float32
    )
    summed_down = reduce_bucket(term_down)
    total_tokens = tokens.shape[0] * lax.axis_size("row") * lax.axis_size("col")
    factor = 1.0 / math.sqrt(total_tokens)
    return (summed_up * factor, summed_down * factor)


def solution(mesh):
    placed = (P(("row", "col"), None), P(("row", "col"), None), P(), P())
    return jax.shard_map(
        local,
        mesh=mesh,
        in_specs=placed,
        out_specs=(P("row", "col"), P("row", "col")),
        check_vma=False,
    )
```

profile of v0, /device:TPU:0, one launch (start us, length us, event | category | flops | bytes accessed | tf_op | source)
XLA Modules:
  0.0 238.0 jit_solution(13804704943461019610)
XLA Ops:
  7.2 0.0 reduce-scatter.5.cloned.1.call-start
  7.2 0.0 copy-start
  7.2 7.6 %fusion.9 = f32[512,512]{1,0:T(8,128)S(1)} fusion(bf16[512,6144]{1,0:T(8,128)(2,1)} %param.4, bf16[6144,512]{1,0:T(8,128)(2,1)} %param.6), kind=kOutput, calls=%fused_computation.19 | convolution fusion | flops 3221225472 | bytes 13631488 | tf_op jit(solution)/shard_map/dot_general | solution.py:28
  14.8 0.0 copy-done
  14.8 3.9 %convolution_convert_fusion = bf16[512,6144]{1,0:T(8,128)(2,1)S(1)} fusion(bf16[512,6144]{1,0:T(8,128)(2,1)S(1)} %copy-done, f32[512,512]{1,0:T(8,128)S(1)} %fusion.9), kind=kOutput, calls=%fused_computation.2 | convolution fusion | flops 3225681920 | bytes 13631488 | tf_op jit(solution)/shard_map/dot_general | solution.py:39
  18.7 75.3 %all_to_all.10 = bf16[6144,4,128]{0,2,1:T(8,128)(2,1)S(1)} all-to-all(bf16[6144,4,128]{0,2,1:T(8,128)(2,1)S(1)} %bitcast.12), channel_id=1, replica_groups=mesh['row'=8,'col'=4] {'col'}, dimensions={1} | all-to-all | bytes 12582912 | tf_op jit(solution)/shard_map/all_to_all | solution.py:20
  94.1 2.9 %convert_reduce_fusion = f32[6144,128]{0,1:T(8,128)} fusion(bf16[6144,4,128]{0,2,1:T(8,128)(2,1)S(1)} %all_to_all.10), kind=kLoop, calls=%fused_computation | loop fusion | flops 5505024 | bytes 9437184 | tf_op jit(solution)/shard_map/reduce_sum | solution.py:23
  96.9 0.0 reduce-scatter.5.cloned.1.call-update
  97.0 0.0 reduce-scatter.3.cloned.1.call-start
  97.0 16.3 %convolution_convert_fusion.1 = bf16[512,6144]{1,0:T(8,128)(2,1)} fusion(bf16[512,6144]{1,0:T(8,128)(2,1)} %param.4, bf16[512,6144]{1,0:T(8,128)(2,1)} %param.5, bf16[512,6144]{1,0:T(8,128)(2,1)} %param.7, f32[512,512]{1,0:T(8,128)S(1)} %fusion.9), kind=kOutput, calls=%fused_computation.3 | convolution fusion | flops 6448218112 | bytes 26214400 | tf_op jit(solution)/shard_map/dot_general | solution.py:35
  113.3 72.8 %all_to_all.11 = bf16[6144,4,128]{0,2,1:T(8,128)(2,1)S(1)} all-to-all(bf16[6144,4,128]{0,2,1:T(8,128)(2,1)} %bitcast.13), channel_id=1, replica_groups=mesh['row'=8,'col'=4] {'col'}, dimensions={1} | all-to-all | bytes 12582912 | tf_op jit(solution)/shard_map/all_to_all | solution.py:20
  186.1 2.8 %convert_reduce_fusion.1 = f32[6144,128]{0,1:T(8,128)} fusion(bf16[6144,4,128]{0,2,1:T(8,128)(2,1)S(1)} %all_to_all.11), kind=kLoop, calls=%fused_computation.1 | loop fusion | flops 5505024 | bytes 9437184 | tf_op jit(solution)/shard_map/reduce_sum | solution.py:23
  188.9 0.0 reduce-scatter.3.cloned.1.call-update
  189.0 0.0 reduce-scatter.5.cloned.1.call-done
  189.0 1.0 broadcast_multiply_fusion
  190.0 0.9 copy.7
  190.9 38.3 %reduce-scatter.3.cloned.1.call-done = f32[768,128]{0,1:T(8,128)} async-done(((f32[6144,128]{0,1:T(8,128)}), f32[768,128]{0,1:T(8,128)}) %reduce-scatter.3.cloned.1.call-update) | async-done | bytes 393232 | tf_op jit(solution)/shard_map/reduce_scatter | solution.py:24
  229.2 1.0 broadcast_multiply_fusion.1
  230.2 0.9 copy.6
Async XLA Ops:
  7.2 181.8 %reduce-scatter.5.cloned.1.call-start = ((), (), s32[]{:S(2)}) async-start(), calls=%async_computation.5 | async-start | bytes 3538944 | tf_op jit(solution)/shard_map/reduce_scatter | solution.py:24
  7.2 7.6 %copy-start = (bf16[512,6144]{1,0:T(8,128)(2,1)S(1)}, bf16[512,6144]{1,0:T(8,128)(2,1)}, u32[]{:S(2)}) copy-start(bf16[512,6144]{1,0:T(8,128)(2,1)} %param.5) | copy-start | bytes 18874372
  97.0 132.3 %reduce-scatter.3.cloned.1.call-start = ((), (), s32[]{:S(2)}) async-start(), calls=%async_computation.4 | async-start | bytes 3538944 | tf_op jit(solution)/shard_map/reduce_scatter | solution.py:24
Sparse Core Ops, SparseCore 0:
  97.1 40.0 reduce-scatter.4
  189.1 40.0 reduce-scatter.2
where the time goes:
time: 238 us
  blocking collectives  148 us (62%)
  waiting for transfers between devices  38.3 us (16%)
  matrix products  27.8 us (12%)
  between operations  14.1 us (6%)
  other arithmetic  7.75 us (3%)
    all_to_all x2, blocking collectives, reduce_bucket(): lax.all_to_all(levels.reshape(rows, col_count, piece_cols), 'col', split_...  148 us
    reduce_scatter x2, waiting for transfers between devices, reduce_bucket(): return lax.psum_scatter(partial_sum, 'row', scatter_dimension=0, tiled=True)  38.3 us
    dot_general x1, matrix products, local(): lax.dot_general(tokens, hidden_grad, (((0,), (0,)), ((), ())), preferred_...  16.3 us
    dot_general x1, matrix products, local(): preact = jnp.dot(tokens, w_up, preferred_element_type=jnp.float32)  7.6 us
    reduce_sum x2, other arithmetic, reduce_bucket(): partial_sum = jnp.sum(got_levels, axis=1, dtype=jnp.float32)  5.7 us
  transfers between devices with their start and end apart: 2, of which 1 were waited for; matrix products, arithmetic and copies ran while one was open for 9% of the time, Pallas kernels for 0%

commit v1 on v0

v1 whole, which is shorter than its diff:
```python
import functools
import math

import jax
import jax.numpy as jnp
from jax import lax
from jax.experimental import pallas as pl
from jax.experimental.pallas import tpu as pltpu
from jax.sharding import PartitionSpec as P

MESH = pl.DeviceIdType.MESH
F32 = jnp.float32
BF16 = jnp.bfloat16


def gelu_parts(preact):
    cumul = 0.5 * (1.0 + lax.erf(preact * (1.0 / math.sqrt(2.0))))
    density = jnp.exp(-0.5 * preact * preact) * (1.0 / math.sqrt(2.0 * math.pi))
    return (preact * cumul, cumul + preact * density)


def kernel(A, B, Z, tok_hbm, grad_hbm, wup_hbm, wdn_hbm, out_down, out_up,
           wide, oth, wu, wd, acc, acc2, slope, lhs, term,
           r1d, r1u, q2d, q2u, r2d, r2u, q3, r3,
           ld, cs, cr, ls, lr, s1d, s1u, g1d, g1u, s2d, s2u, g2d, g2u, s3, g3):
    T, D = tok_hbm.shape
    C = wup_hbm.shape[1]
    db = D // (2 * Z)
    cb = C // (A * B)
    nt = 256 if db % 256 == 0 else 128
    row, col = lax.axis_index("row"), lax.axis_index("col")
    core, z = lax.rem(row, 2), row // 2
    a, b = lax.rem(col, A), col // A

    def at(b_, a_):
        return (row, b_ * A + a_)

    peer = (z * 2 + (1 - core), col)

    def cols(k, c):
        return pl.ds(pl.multiple_of((2 * k + c) * db, db), db)

    def load_first(k):
        return [
            pltpu.make_async_copy(tok_hbm.at[:, cols(k, core)], wide.at[1, k, pl.ds(0, T)], ld.at[0, k]),
            pltpu.make_async_copy(wup_hbm.at[cols(k, core)], wu.at[k, 0], ld.at[1, k]),
            pltpu.make_async_copy(tok_hbm.at[:, cols(k, 1 - core)], oth.at[1, k], ld.at[2, k]),
            pltpu.make_async_copy(wup_hbm.at[cols(k, 1 - core)], wu.at[k, 1], ld.at[3, k]),
        ]

    def load_second(k):
        return [
            pltpu.make_async_copy(grad_hbm.at[:, cols(k, core)], wide.at[0, k, pl.ds(0, T)], ld.at[4, k]),
            pltpu.make_async_copy(wdn_hbm.at[:, cols(k, core)], wd.at[k, 0], ld.at[5, k]),
            pltpu.make_async_copy(grad_hbm.at[:, cols(k, 1 - core)], oth.at[0, k], ld.at[6, k]),
            pltpu.make_async_copy(wdn_hbm.at[:, cols(k, 1 - core)], wd.at[k, 1], ld.at[7, k]),
        ]

    for k in range(Z):
        for copy in load_first(k):
            copy.start()

    barrier = pltpu.get_barrier_semaphore()
    partners = [peer]
    partners += [at(b, lax.rem(a + d, A)) for d in range(1, A)]
    partners += [at(lax.rem(b + d, B), a) for d in range(1, B)]
    partners += [(lax.rem(z + d, Z) * 2 + core, col) for d in range(1, Z)]
    for partner in partners:
        pl.semaphore_signal(barrier, inc=1, device_id=partner, device_id_type=MESH)
    pl.semaphore_wait(barrier, len(partners))

    def swap(bucket, k):
        source = (grad_hbm, tok_hbm)[bucket]
        return pltpu.make_async_remote_copy(
            source.at[:, cols(k, 1 - core)], wide.at[bucket, k, pl.ds(T, T)],
            cs.at[bucket, k], cr.at[bucket, k], device_id=peer, device_id_type=MESH)

    def swap_lhs(bucket):
        return pltpu.make_async_remote_copy(
            lhs.at[bucket, :, pl.ds(0, T)], lhs.at[bucket, :, pl.ds(T, T)],
            ls.at[bucket], lr.at[bucket], device_id=peer, device_id_type=MESH)

    def block(t):
        return lax.rem(z + 1 + t, Z)

    for t in range(Z):
        swap(0, block(t)).start()
    for k in range(Z):
        for copy in load_second(k):
            copy.start()
    for t in range(Z):
        swap(1, block(t)).start()

    acc[...] = jnp.zeros_like(acc)

    def preact_step(k, carry):
        for copy in load_first(k):
            copy.wait()
        acc[...] += (jnp.dot(wide[1, k, :T], wu[k, 0], preferred_element_type=F32)
                     + jnp.dot(oth[1, k], wu[k, 1], preferred_element_type=F32))
        return carry

    lax.fori_loop(0, Z, preact_step, 0)

    def gelu_step(i, carry):
        part = pl.ds(pl.multiple_of(i * 128, 128), 128)
        value, steep = gelu_parts(acc[:, part].T)
        lhs[0, part, :T] = value.astype(BF16)
        slope[part, :] = steep
        return carry

    lax.fori_loop(0, C // 128, gelu_step, 0)
    swap_lhs(0).start()

    acc2[...] = jnp.zeros_like(acc2)
    across = (((1,), (1,)), ((), ()))

    def grad_step(k, carry):
        for copy in load_second(k):
            copy.wait()
        acc2[...] += (lax.dot_general(wd[k, 0], wide[0, k, :T], across, preferred_element_type=F32)
                      + lax.dot_general(wd[k, 1], oth[0, k], across, preferred_element_type=F32))
        return carry

    lax.fori_loop(0, Z, grad_step, 0)
    lhs[1, :, :T] = (acc2[...] * slope[...]).astype(BF16)
    swap_lhs(1).start()

    def send1(bucket, t):
        if bucket == 0:
            return [pltpu.make_async_remote_copy(
                term.at[0, t, lax.rem(b + d, B)], r1d.at[t, d - 1], s1d.at[t, d - 1], g1d.at[t, d - 1],
                device_id=at(lax.rem(b + d, B), a), device_id_type=MESH) for d in range(1, B)]
        return [pltpu.make_async_remote_copy(
            term.at[1, t, :, lax.rem(a + d, A)], r1u.at[t, d - 1], s1u.at[t, d - 1], g1u.at[t, d - 1],
            device_id=at(b, lax.rem(a + d, A)), device_id_type=MESH) for d in range(1, A)]

    def send2(bucket, t):
        if bucket == 0:
            return [pltpu.make_async_remote_copy(
                q2d.at[t, d - 1], r2d.at[t, d - 1], s2d.at[t, d - 1], g2d.at[t, d - 1],
                device_id=at(b, lax.rem(a + d, A)), device_id_type=MESH) for d in range(1, A)]
        return [pltpu.make_async_remote_copy(
            q2u.at[t, d - 1], r2u.at[t, d - 1], s2u.at[t, d - 1], g2u.at[t, d - 1],
            device_id=at(lax.rem(b + d, B), a), device_id_type=MESH) for d in range(1, B)]

    def send3(bucket, t):
        return pltpu.make_async_remote_copy(
            q3.at[bucket, t], r3.at[bucket, t], s3.at[bucket, t], g3.at[bucket, t],
            device_id=(block(t) * 2 + core, col), device_id_type=MESH)

    def sum1(bucket, t, b_, a_):
        total = term[bucket, t, b_, a_].astype(F32)
        if bucket == 0:
            for d in range(B - 1):
                total += r1d[t, d, a_].astype(F32)
        else:
            for d in range(A - 1):
                total += r1u[t, d, b_].astype(F32)
        return total

    def sum2(bucket, t):
        total = sum1(bucket, t, b, a)
        got, count = ((r2d, A - 1), (r2u, B - 1))[bucket]
        for d in range(count):
            total += got[t, d].astype(F32)
        return total

    def start1(t):
        for bucket in range(2):
            for copy in send1(bucket, t):
                copy.start()

    def term_step(t, carry):
        k = block(t)
        for bucket in range(2):
            swap(bucket, k).wait_recv()

            @pl.when(t == 0)
            def _():
                swap_lhs(bucket).wait_recv()

            for n in range(0, db, nt):
                out = jnp.dot(lhs[bucket], wide[bucket, k, :, n:n + nt], preferred_element_type=F32)
                term[bucket, t, :, :, :, n:n + nt] = out.astype(BF16).reshape(B, A, cb, nt)

            @pl.when(t < 2)
            def _():
                for copy in send1(bucket, t):
                    copy.start()
        return carry

    lax.fori_loop(0, Z, term_step, 0)

    def finish2(t):
        for bucket in range(2):
            for copy in send2(bucket, t):
                copy.wait_recv()
            if t < Z - 1:
                q3[bucket, t] = sum2(bucket, t).astype(BF16)
                send3(bucket, t).start()

    for t in range(Z):
        for bucket in range(2):
            for copy in send1(bucket, t):
                copy.wait_recv()
            if bucket == 0:
                for d in range(1, A):
                    q2d[t, d - 1] = sum1(0, t, b, lax.rem(a + d, A)).astype(BF16)
            else:
                for d in range(1, B):
                    q2u[t, d - 1] = sum1(1, t, lax.rem(b + d, B), a).astype(BF16)
            for copy in send2(bucket, t):
                copy.start()
        if t + 2 < Z - 1:
            start1(t + 2)
        if t == Z - 2 and Z - 1 >= 2:
            start1(Z - 1)
        if t >= 1:
            finish2(t - 1)
    finish2(Z - 1)

    for bucket, out in enumerate((out_down, out_up)):
        total = sum2(bucket, Z - 1)
        for t in range(Z - 1):
            send3(bucket, t).wait_recv()
            total += r3[bucket, t].astype(F32)
        out[...] = total

    for bucket in range(2):
        swap_lhs(bucket).wait_send()
        for t in range(Z):
            swap(bucket, block(t)).wait_send()
            for copy in send1(bucket, t) + send2(bucket, t):
                copy.wait_send()
            if t < Z - 1:
                send3(bucket, t).wait_send()


def local(A, B, Z, tokens, grad_out, w_up, w_down):
    T, D = tokens.shape
    C = w_up.shape[1]
    db, cb = D // (2 * Z), C // (A * B)
    one = lambda n: max(n, 1)
    dma = lambda *shape: pltpu.SemaphoreType.DMA(shape)
    hop = lambda: [dma(Z, one(B - 1)), dma(Z, one(A - 1))]
    hop2 = lambda: [dma(Z, one(A - 1)), dma(Z, one(B - 1))]
    any_spec = pl.BlockSpec(memory_space=pl.ANY)
    vmem_spec = pl.BlockSpec(memory_space=pltpu.VMEM)
    piece = jax.ShapeDtypeStruct((cb, db), F32)
    down, up = pl.pallas_call(
        functools.partial(kernel, A, B, Z),
        out_shape=(piece, piece),
        in_specs=[any_spec] * 4,
        out_specs=(vmem_spec, vmem_spec),
        scratch_shapes=[
            pltpu.VMEM((2, Z, 2 * T, db), BF16),
            pltpu.VMEM((2, Z, T, db), BF16),
            pltpu.VMEM((Z, 2, db, C), BF16),
            pltpu.VMEM((Z, 2, C, db), BF16),
            pltpu.VMEM((T, C), F32),
            pltpu.VMEM((C, T), F32),
            pltpu.VMEM((C, T), F32),
            pltpu.VMEM((2, C, 2 * T), BF16),
            pltpu.VMEM((2, Z, B, A, cb, db), BF16),
            pltpu.VMEM((Z, one(B - 1), A, cb, db), BF16),
            pltpu.VMEM((Z, one(A - 1), B, cb, db), BF16),
            pltpu.VMEM((Z, one(A - 1), cb, db), BF16),
            pltpu.VMEM((Z, one(B - 1), cb, db), BF16),
            pltpu.VMEM((Z, one(A - 1), cb, db), BF16),
            pltpu.VMEM((Z, one(B - 1), cb, db), BF16),
            pltpu.VMEM((2, one(Z - 1), cb, db), BF16),
            pltpu.VMEM((2, one(Z - 1), cb, db), BF16),
            dma(8, Z), dma(2, Z), dma(2, Z), dma(2), dma(2),
            *hop(), *hop(), *hop2(), *hop2(),
            dma(2, one(Z - 1)), dma(2, one(Z - 1)),
        ],
        compiler_params=pltpu.CompilerParams(
            collective_id=0, has_side_effects=True, vmem_limit_bytes=66000000
        ),
    )(tokens, grad_out, w_up, w_down)
    total_tokens = T * lax.axis_size("row") * lax.axis_size("col")
    factor = 1.0 / math.sqrt(total_tokens)
    return (up.T * factor, down.T * factor)


def solution(mesh):
    rows, columns = mesh.shape["row"], mesh.shape["col"]
    A = 2 if columns % 2 == 0 else 1
    placed = (P(("row", "col"), None), P(("row", "col"), None), P(), P())
    return jax.shard_map(
        functools.partial(local, A, columns // A, rows // 2),
        mesh=mesh,
        in_specs=placed,
        out_specs=(P("row", "col"), P("row", "col")),
        check_vma=False,
    )
```

time: 238 us -> 87.3 us (0.37)
  blocking collectives: 148 us -> 0 us
  Pallas kernels: 0 us -> 83.5 us
  waiting for transfers between devices: 38.3 us -> 0 us
  matrix products: 27.8 us -> 0 us
  between operations: 14.1 us -> 0.64 us
  other arithmetic: 7.75 us -> 1.17 us
    all_to_all x2 -> x0, blocking collectives: 148 us -> none  [reduce_bucket(): lax.all_to_all(levels.reshape(rows, col_count, piece_cols), 'col', split_...]
    pallas_call x0 -> x1, Pallas kernels: none -> 83.5 us  [local(): pl.pallas_call(functools.partial(kernel, A, B, Z), out_shape=(piece, piec...]
    reduce_scatter x2 -> x0, waiting for transfers between devices: 38.3 us -> none  [reduce_bucket(): return lax.psum_scatter(partial_sum, 'row', scatter_dimension=0, tiled=True)]
    dot_general x3 -> x0, matrix products: 27.8 us -> none  [the longest x1 16.3 us: local(): lax.dot_general(tokens, hidden_grad, (((0,), (0,)), ((), ())), preferred_...]
    reduce_sum x2 -> x0, other arithmetic: 5.7 us -> none  [reduce_bucket(): partial_sum = jnp.sum(got_levels, axis=1, dtype=jnp.float32)]
  transfers between devices with their start and end apart: 2 -> 0, of which waited for: 1 -> 0; matrix products, arithmetic and copies ran while one was open for 9% -> 0% of each run, Pallas kernels for 0% -> 0%
where the time goes in v1:
time: 87.3 us; the launch traced here: 87.2 us
  Pallas kernels  83.5 us (96%)
  local copies, waits for them, and re-layouts  1.83 us (2%)
  other arithmetic  1.17 us (1%)
    pallas_call x1, Pallas kernels, local(): pl.pallas_call(functools.partial(kernel, A, B, Z), out_shape=(piece, piec...  83.5 us
    unnamed x2, local copies, waits for them, and re-layouts  1.83 us

profile of v1, /device:TPU:0, one launch (start us, length us, event | category | flops | bytes accessed | tf_op | source)
XLA Modules:
  0.0 87.2 jit_solution(9342861566787554453)
XLA Ops:
  0.6 83.5 %shard_map.59 = (f32[128,768]{1,0:T(8,128)}, f32[128,768]{1,0:T(8,128)}) custom-call(bf16[512,6144]{1,0:T(8,128)(2,1)} %tok_hbm.1, bf16[512,6144]{1,0:T(8,128)(2,1)} %grad_hbm.1, bf16[6144,512]{1,0:T(8,128)(2,1)} %wup_hbm.1, bf16[512,6144]{1,0:T(8,128)(2,1)} %wdn_hbm.1), custom_call_target="tpu_custom_call" | custom-call | tf_op jit(solution)/shard_map/pallas_call | solution.py:251
  84.2 1.2 %multiply_bitcast_fusion = (f32[768,128]{0,1:T(8,128)S(1)}, f32[768,128]{0,1:T(8,128)S(1)}) fusion(f32[128,768]{1,0:T(8,128)} %get-tuple-element.5, f32[128,768]{1,0:T(8,128)} %get-tuple-element.4), kind=kLoop, calls=%fused_computation | loop fusion | flops 196608 | bytes 1572864 | tf_op jit(solution)/shard_map/mul | solution.py:284
  85.4 0.9 %copy.7 = f32[768,128]{1,0:T(8,128)} copy(f32[768,128]{0,1:T(8,128)S(1)} %get-tuple-element.8) | data formatting | bytes 786432
  86.3 0.9 %copy.6 = f32[768,128]{1,0:T(8,128)} copy(f32[768,128]{0,1:T(8,128)S(1)} %get-tuple-element.9) | data formatting | bytes 786432

commit v2 on v1

--- a/solution.py
+++ b/solution.py
@@ -83,6 +83,11 @@
     def block(t):
         return lax.rem(z + 1 + t, Z)
 
+    def chunk(p):
+        if p >= 2 * Z - 2:
+            return p - (2 * Z - 2), Z - 1
+        return p // (Z - 1), p % (Z - 1)
+
     for t in range(Z):
         swap(0, block(t)).start()
     for k in range(Z):
@@ -112,11 +117,77 @@
     lax.fori_loop(0, C // 128, gelu_step, 0)
     swap_lhs(0).start()
 
+    def send1(h, u):
+        if h == 0:
+            return [pltpu.make_async_remote_copy(
+                term.at[2 * u, lax.rem(b + d, B)], r1d.at[u, d - 1], s1d.at[u, d - 1], g1d.at[u, d - 1],
+                device_id=at(lax.rem(b + d, B), a), device_id_type=MESH) for d in range(1, B)]
+        return [pltpu.make_async_remote_copy(
+            term.at[2 * u + 1, :, lax.rem(a + d, A)], r1u.at[u, d - 1], s1u.at[u, d - 1], g1u.at[u, d - 1],
+            device_id=at(b, lax.rem(a + d, A)), device_id_type=MESH) for d in range(1, A)]
+
+    def send2(h, u):
+        if h == 0:
+            return [pltpu.make_async_remote_copy(
+                q2d.at[u, d - 1], r2d.at[u, d - 1], s2d.at[u, d - 1], g2d.at[u, d - 1],
+                device_id=at(b, lax.rem(a + d, A)), device_id_type=MESH) for d in range(1, A)]
+        return [pltpu.make_async_remote_copy(
+            q2u.at[u, d - 1], r2u.at[u, d - 1], s2u.at[u, d - 1], g2u.at[u, d - 1],
+            device_id=at(lax.rem(b + d, B), a), device_id_type=MESH) for d in range(1, B)]
+
+    def send3(bucket, t):
+        return pltpu.make_async_remote_copy(
+            q3.at[bucket, t], r3.at[bucket, t], s3.at[bucket, t], g3.at[bucket, t],
+            device_id=(block(t) * 2 + core, col), device_id_type=MESH)
+
+    def sum1(h, u, b_, a_):
+        total = term[2 * u + h, b_, a_].astype(F32)
+        if h == 0:
+            for d in range(B - 1):
+                total += r1d[u, d, a_].astype(F32)
+        else:
+            for d in range(A - 1):
+                total += r1u[u, d, b_].astype(F32)
+        return total
+
+    def sum2(h, u):
+        total = sum1(h, u, b, a)
+        got, count = ((r2d, A - 1), (r2u, B - 1))[h]
+        for d in range(count):
+            total += got[u, d].astype(F32)
+        return total
+
+    def term_of(bucket):
+        swap_lhs(bucket).wait_recv()
+
+        def term_step(t, p):
+            k = block(t)
+            swap(bucket, k).wait_recv()
+            if bucket == 0:
+                load_second(k)[0].wait()
+            for n in range(0, db, nt):
+                out = jnp.dot(lhs[bucket], wide[bucket, k, :, n:n + nt], preferred_element_type=F32)
+                term[p, :, :, :, n:n + nt] = out.astype(BF16).reshape(B, A, cb, nt)
+            for h in range(2):
+                @pl.when((p < 4) & (lax.rem(p, 2) == h))
+                def _():
+                    for copy in send1(h, p // 2):
+                        copy.start()
+
+        def loop_step(t, carry):
+            term_step(t, bucket * (Z - 1) + t)
+            return carry
+
+        lax.fori_loop(0, Z - 1, loop_step, 0)
+        term_step(Z - 1, 2 * Z - 2 + bucket)
+
+    term_of(0)
+
     acc2[...] = jnp.zeros_like(acc2)
     across = (((1,), (1,)), ((), ()))
 
     def grad_step(k, carry):
-        for copy in load_second(k):
+        for copy in load_second(k)[1:]:
             copy.wait()
         acc2[...] += (lax.dot_general(wd[k, 0], wide[0, k, :T], across, preferred_element_type=F32)
                       + lax.dot_general(wd[k, 1], oth[0, k], across, preferred_element_type=F32))
@@ -125,116 +196,63 @@
     lax.fori_loop(0, Z, grad_step, 0)
     lhs[1, :, :T] = (acc2[...] * slope[...]).astype(BF16)
     swap_lhs(1).start()
-
-    def send1(bucket, t):
-        if bucket == 0:
-            return [pltpu.make_async_remote_copy(
-                term.at[0, t, lax.rem(b + d, B)], r1d.at[t, d - 1], s1d.at[t, d - 1], g1d.at[t, d - 1],
-                device_id=at(lax.rem(b + d, B), a), device_id_type=MESH) for d in range(1, B)]
-        return [pltpu.make_async_remote_copy(
-            term.at[1, t, :, lax.rem(a + d, A)], r1u.at[t, d - 1], s1u.at[t, d - 1], g1u.at[t, d - 1],
-            device_id=at(b, lax.rem(a + d, A)), device_id_type=MESH) for d in range(1, A)]
-
-    def send2(bucket, t):
-        if bucket == 0:
-            return [pltpu.make_async_remote_copy(
-                q2d.at[t, d - 1], r2d.at[t, d - 1], s2d.at[t, d - 1], g2d.at[t, d - 1],
-                device_id=at(b, lax.rem(a + d, A)), device_id_type=MESH) for d in range(1, A)]
-        return [pltpu.make_async_remote_copy(
-            q2u.at[t, d - 1], r2u.at[t, d - 1], s2u.at[t, d - 1], g2u.at[t, d - 1],
-            device_id=at(lax.rem(b + d, B), a), device_id_type=MESH) for d in range(1, B)]
-
-    def send3(bucket, t):
-        return pltpu.make_async_remote_copy(
-            q3.at[bucket, t], r3.at[bucket, t], s3.at[bucket, t], g3.at[bucket, t],
-            device_id=(block(t) * 2 + core, col), device_id_type=MESH)
-
-    def sum1(bucket, t, b_, a_):
-        total = term[bucket, t, b_, a_].astype(F32)
-        if bucket == 0:
-            for d in range(B - 1):
-                total += r1d[t, d, a_].astype(F32)
+    term_of(1)
+
+    def step1(h, u):
+        for copy in send1(h, u):
+            copy.wait_recv()
+        if h == 0:
+            for d in range(1, A):
+                q2d[u, d - 1] = sum1(0, u, b, lax.rem(a + d, A)).astype(BF16)
         else:
-            for d in range(A - 1):
-                total += r1u[t, d, b_].astype(F32)
-        return total
-
-    def sum2(bucket, t):
-        total = sum1(bucket, t, b, a)
-        got, count = ((r2d, A - 1), (r2u, B - 1))[bucket]
-        for d in range(count):
-            total += got[t, d].astype(F32)
-        return total
-
-    def start1(t):
-        for bucket in range(2):
-            for copy in send1(bucket, t):
-                copy.start()
-
-    def term_step(t, carry):
-        k = block(t)
-        for bucket in range(2):
-            swap(bucket, k).wait_recv()
-
-            @pl.when(t == 0)
-            def _():
-                swap_lhs(bucket).wait_recv()
-
-            for n in range(0, db, nt):
-                out = jnp.dot(lhs[bucket], wide[bucket, k, :, n:n + nt], preferred_element_type=F32)
-                term[bucket, t, :, :, :, n:n + nt] = out.astype(BF16).reshape(B, A, cb, nt)
-
-            @pl.when(t < 2)
-            def _():
-                for copy in send1(bucket, t):
+            for d in range(1, B):
+                q2u[u, d - 1] = sum1(1, u, lax.rem(b + d, B), a).astype(BF16)
+        for copy in send2(h, u):
+            copy.start()
+
+    def step2(h, u):
+        for copy in send2(h, u):
+            copy.wait_recv()
+        bucket, t = chunk(2 * u + h)
+        if t < Z - 1:
+            q3[bucket, t] = sum2(h, u).astype(BF16)
+            send3(bucket, t).start()
+
+    def start1(u):
+        if 2 <= u < Z:
+            for h in range(2):
+                for copy in send1(h, u):
                     copy.start()
-        return carry
-
-    lax.fori_loop(0, Z, term_step, 0)
-
-    def finish2(t):
-        for bucket in range(2):
-            for copy in send2(bucket, t):
-                copy.wait_recv()
-            if t < Z - 1:
-                q3[bucket, t] = sum2(bucket, t).astype(BF16)
-                send3(bucket, t).start()
-
-    for t in range(Z):
-        for bucket in range(2):
-            for copy in send1(bucket, t):
-                copy.wait_recv()
-            if bucket == 0:
-                for d in range(1, A):
-                    q2d[t, d - 1] = sum1(0, t, b, lax.rem(a + d, A)).astype(BF16)
-            else:
-                for d in range(1, B):
-                    q2u[t, d - 1] = sum1(1, t, lax.rem(b + d, B), a).astype(BF16)
-            for copy in send2(bucket, t):
-                copy.start()
-        if t + 2 < Z - 1:
-            start1(t + 2)
-        if t == Z - 2 and Z - 1 >= 2:
+
+    for u in range(Z):
+        if u >= 1 and u == Z - 1:
+            for h in range(2):
+                step2(h, u - 1)
+        for h in range(2):
+            step1(h, u)
+        if u + 2 < Z - 1:
+            start1(u + 2)
+        if u == Z - 2:
             start1(Z - 1)
-        if t >= 1:
-            finish2(t - 1)
-    finish2(Z - 1)
-
-    for bucket, out in enumerate((out_down, out_up)):
-        total = sum2(bucket, Z - 1)
+        if u >= 1 and u < Z - 1:
+            for h in range(2):
+                step2(h, u - 1)
+    for h, out in enumerate((out_down, out_up)):
+        step2(h, Z - 1)
+        total = sum2(h, Z - 1)
         for t in range(Z - 1):
-            send3(bucket, t).wait_recv()
-            total += r3[bucket, t].astype(F32)
-        out[...] = total
-
-    for bucket in range(2):
-        swap_lhs(bucket).wait_send()
+            send3(h, t).wait_recv()
+            total += r3[h, t].astype(F32)
+        out[...] = total.T
+
+    for h in range(2):
+        swap_lhs(h).wait_send()
         for t in range(Z):
-            swap(bucket, block(t)).wait_send()
-            for copy in send1(bucket, t) + send2(bucket, t):
+            swap(h, block(t)).wait_send()
+            for copy in send1(h, t) + send2(h, t):
                 copy.wait_send()
             if t < Z - 1:
-                send3(bucket, t).wait_send()
+                send3(h, t).wait_send()
 
 
 def local(A, B, Z, tokens, grad_out, w_up, w_down):
@@ -247,7 +265,7 @@
     hop2 = lambda: [dma(Z, one(A - 1)), dma(Z, one(B - 1))]
     any_spec = pl.BlockSpec(memory_space=pl.ANY)
     vmem_spec = pl.BlockSpec(memory_space=pltpu.VMEM)
-    piece = jax.ShapeDtypeStruct((cb, db), F32)
+    piece = jax.ShapeDtypeStruct((db, cb), F32)
     down, up = pl.pallas_call(
         functools.partial(kernel, A, B, Z),
         out_shape=(piece, piece),
@@ -262,7 +280,7 @@
             pltpu.VMEM((C, T), F32),
             pltpu.VMEM((C, T), F32),
             pltpu.VMEM((2, C, 2 * T), BF16),
-            pltpu.VMEM((2, Z, B, A, cb, db), BF16),
+            pltpu.VMEM((2 * Z, B, A, cb, db), BF16),
             pltpu.VMEM((Z, one(B - 1), A, cb, db), BF16),
             pltpu.VMEM((Z, one(A - 1), B, cb, db), BF16),
             pltpu.VMEM((Z, one(A - 1), cb, db), BF16),
@@ -281,7 +299,7 @@
     )(tokens, grad_out, w_up, w_down)
     total_tokens = T * lax.axis_size("row") * lax.axis_size("col")
     factor = 1.0 / math.sqrt(total_tokens)
-    return (up.T * factor, down.T * factor)
+    return (up * factor, down * factor)
 
 
 def solution(mesh):

time: 87.3 us -> 78.6 us (0.900)
  Pallas kernels: 83.5 us -> 75.7 us
  local copies, waits for them, and re-layouts: 1.83 us -> 0 us
    pallas_call x1, Pallas kernels: 83.5 us -> 75.7 us  [local(): pl.pallas_call(functools.partial(kernel, A, B, Z), out_shape=(piece, piec...]
    unnamed x2 -> x0, local copies, waits for them, and re-layouts: 1.83 us -> none
    mul x1, other arithmetic: 1.17 us -> 2.04 us  [local(): return (up * factor, down * factor)]
where the time goes in v2:
time: 78.6 us; the launch traced here: 78.3 us
  Pallas kernels  75.7 us (96%)
  other arithmetic  2.04 us (3%)
    pallas_call x1, Pallas kernels, local(): pl.pallas_call(functools.partial(kernel, A, B, Z), out_shape=(piece, piec...  75.7 us
    mul x1, other arithmetic, local(): return (up * factor, down * factor)  2.04 us

profile of v2, /device:TPU:0, one launch (start us, length us, event | category | flops | bytes accessed | tf_op | source)
XLA Modules:
  0.0 78.3 jit_solution(6382035068854724843)
XLA Ops:
  0.6 75.7 %shard_map.59 = (f32[768,128]{1,0:T(8,128)}, f32[768,128]{1,0:T(8,128)}) custom-call(bf16[512,6144]{1,0:T(8,128)(2,1)} %tok_hbm.1, bf16[512,6144]{1,0:T(8,128)(2,1)} %grad_hbm.1, bf16[6144,512]{1,0:T(8,128)(2,1)} %wup_hbm.1, bf16[512,6144]{1,0:T(8,128)(2,1)} %wdn_hbm.1), custom_call_target="tpu_custom_call" | custom-call | tf_op jit(solution)/shard_map/pallas_call | solution.py:269
  76.3 2.0 %broadcast_multiply_fusion = (f32[768,128]{1,0:T(8,128)}, f32[768,128]{1,0:T(8,128)}) fusion(f32[768,128]{1,0:T(8,128)} %get-tuple-element.5, f32[768,128]{1,0:T(8,128)} %get-tuple-element.4), kind=kLoop, calls=%fused_computation | loop fusion | flops 196608 | bytes 1572864 | tf_op jit(solution)/shard_map/mul | solution.py:302

commit v3 on v2

--- a/solution.py
+++ b/solution.py
@@ -60,6 +60,10 @@
         for copy in load_first(k):
             copy.start()
 
+    for k in range(Z):
+        for copy in load_second(k):
+            copy.start()
+
     barrier = pltpu.get_barrier_semaphore()
     partners = [peer]
     partners += [at(b, lax.rem(a + d, A)) for d in range(1, A)]
@@ -90,9 +94,6 @@
 
     for t in range(Z):
         swap(0, block(t)).start()
-    for k in range(Z):
-        for copy in load_second(k):
-            copy.start()
     for t in range(Z):
         swap(1, block(t)).start()
 

time: 78.6 us -> 78.7 us (level)
  no operation moved by 1% of the time
where the time goes in v3:
time: 78.7 us; the launch traced here: 78.4 us
  Pallas kernels  75.7 us (96%)
  other arithmetic  2.04 us (3%)
    pallas_call x1, Pallas kernels, local(): pl.pallas_call(functools.partial(kernel, A, B, Z), out_shape=(piece, piec...  75.7 us
    mul x1, other arithmetic, local(): return (up * factor, down * factor)  2.04 us

profile of v3, /device:TPU:0, one launch (start us, length us, event | category | flops | bytes accessed | tf_op | source)
XLA Modules:
  0.0 78.4 jit_solution(12410724439712041841)
XLA Ops:
  0.6 75.7 %shard_map.59 = (f32[768,128]{1,0:T(8,128)}, f32[768,128]{1,0:T(8,128)}) custom-call(bf16[512,6144]{1,0:T(8,128)(2,1)} %tok_hbm.1, bf16[512,6144]{1,0:T(8,128)(2,1)} %grad_hbm.1, bf16[6144,512]{1,0:T(8,128)(2,1)} %wup_hbm.1, bf16[512,6144]{1,0:T(8,128)(2,1)} %wdn_hbm.1), custom_call_target="tpu_custom_call" | custom-call | tf_op jit(solution)/shard_map/pallas_call | solution.py:270
  76.3 2.0 %broadcast_multiply_fusion = (f32[768,128]{1,0:T(8,128)}, f32[768,128]{1,0:T(8,128)}) fusion(f32[768,128]{1,0:T(8,128)} %get-tuple-element.5, f32[768,128]{1,0:T(8,128)} %get-tuple-element.4), kind=kLoop, calls=%fused_computation | loop fusion | flops 196608 | bytes 1572864 | tf_op jit(solution)/shard_map/mul | solution.py:303
